TPU v7x, 8 devices: a whole 2x2x1 slice. The times are simulated.
8 devices in a mesh: side: 2 (over z, y), rep: 4 (over x, core).
Axes of the slice: x: 2, y: 2, z: 1, core: 2. Of those that a mesh axis runs over, the one named last changes fastest.
Arguments:
- w_up: float32 [2, 1, 1536, 8960], P('side', None, 'rep')
- w_down: float32 [2, 1, 8960, 1536], P('side', None, None, 'rep')
- g_up: float32 [2, 1, 1536, 8960], P('side', None, 'rep')
- g_down: float32 [2, 1, 8960, 1536], P('side', None, None, 'rep')
- learn_rate: float32 [1], replicated
- old_up: bfloat16 [2, 4, 1, 1536, 8960], P('side', 'rep')
- old_down: bfloat16 [2, 4, 1, 8960, 1536], P('side', 'rep')
- prompts: bfloat16 [2, 4, 8192, 1536], P('side', 'rep')
Outputs:
- output 1: float32 [2, 1, 1536, 8960], P('side', None, 'rep')
- output 2: float32 [2, 1, 8960, 1536], P('side', None, None, 'rep')
- output 3: bfloat16 [2, 4, 8192, 1536], P('side', 'rep')
All inputs are finite; a program needn't handle non-finite values.
Results may differ from a plain program's by a relative error of at most 0.001.
Values are sent between devices in bfloat16 or wider.
A program may use at most 1 GiB of HBM per device.

v0:
```python
import jax
import jax.numpy as jnp
from jax import lax
from jax.sharding import PartitionSpec as P


def solution(mesh):
    tp_width = mesh.shape["side"] // 2
    send_pairs = [(slot_pos, slot_pos + tp_width) for slot_pos in range(tp_width)]
    up_spec = P("side", None, "rep", None)
    down_spec = P("side", None, None, "rep")
    copy_spec = P("side", "rep", None, None, None)
    token_spec = P("side", "rep", None, None)

    def local_step(w_up, w_down, g_up, g_down, learn_rate, old_up, old_down, prompts):
        step_rate = learn_rate[0]
        new_up = w_up - step_rate * g_up
        new_down = w_down - step_rate * g_down
        delta_up = (new_up - w_up)[0].astype(jnp.bfloat16)
        delta_down = (new_down - w_down)[0].astype(jnp.bfloat16)
        recv_up = lax.ppermute(delta_up, "side", send_pairs)
        recv_down = lax.ppermute(delta_down, "side", send_pairs)
        full_up = lax.all_gather(recv_up, "rep", axis=1, tiled=True)
        full_down = lax.all_gather(recv_down, "rep", axis=2, tiled=True)
        gen_up = (old_up[0, 0].astype(jnp.float32) + full_up.astype(jnp.float32)).astype(jnp.bfloat16)
        gen_down = (old_down[0, 0].astype(jnp.float32) + full_down.astype(jnp.float32)).astype(jnp.bfloat16)
        is_gen = lax.axis_index("side") >= tp_width
        gen_mask = is_gen.astype(jnp.float32)
        hidden = prompts[0, 0]
        for layer_idx in range(w_up.shape[1]):
            pre_act = jnp.dot(hidden, gen_up[layer_idx], preferred_element_type=jnp.float32)
            act_val = jax.nn.gelu(pre_act, approximate=False).astype(jnp.bfloat16)
            part_sum = jnp.dot(act_val, gen_down[layer_idx], preferred_element_type=jnp.float32)
            tp_total = lax.psum(part_sum * gen_mask, "side")
            hidden = (hidden.astype(jnp.float32) + tp_total).astype(jnp.bfloat16)
        y_local = jnp.where(is_gen, hidden, jnp.zeros_like(hidden))
        return new_up, new_down, y_local[None, None]

    return jax.shard_map(
        local_step,
        mesh=mesh,
        in_specs=(up_spec, down_spec, up_spec, down_spec, P(None), copy_spec, copy_spec, token_spec),
        out_specs=(up_spec, down_spec, token_spec),
        check_vma=False,
    )
```

profile of v0, /device:TPU:4, one launch (start us, length us, event | category | flops | bytes accessed | tf_op | source)
XLA Modules:
  0.0 2562.9 jit_solution(8340909114190373005)
XLA Ops:
  7.2 0.0 all-gather.3.cloned.1.call-start
  7.9 14.7 fusion.39
  22.5 1.3 collective-permute-start
  23.8 150.5 %collective-permute-done = bf16[1,384,8960]{2,1,0:T(8,128)(2,1)} collective-permute-done((bf16[1,384,8960]{2,1,0:T(8,128)(2,1)S(1)}, bf16[1,384,8960]{2,1,0:T(8,128)(2,1)}, u32[]{:S(2)}, u32[]{:S(2)}) %collective-permute-start) | collective-permute-done | bytes 6881312 | tf_op jit(solution)/shard_map/ppermute | solution.py:21
  174.3 0.0 all-gather.3.cloned.1.call-update
  174.3 0.0 all-gather.5.cloned.1.call-start
  174.4 16.2 fusion.40
  190.6 1.3 collective-permute-start.1
  191.9 149.7 %collective-permute-done.1 = bf16[1,8960,384]{2,1,0:T(8,128)(2,1)} collective-permute-done((bf16[1,8960,384]{2,1,0:T(8,128)(2,1)}, bf16[1,8960,384]{2,1,0:T(8,128)(2,1)}, u32[]{:S(2)}, u32[]{:S(2)}) %collective-permute-start.1) | collective-permute-done | bytes 6881312 | tf_op jit(solution)/shard_map/ppermute | solution.py:22
  341.6 0.0 all-gather.5.cloned.1.call-update
  341.6 0.0 all-reduce.2.cloned.1.call-start
  341.7 0.0 all-gather.3.cloned.1.call-done
  341.7 835.3 %fusion.85 = bf16[8192,8960]{0,1:T(8,128)(2,1)} fusion(bf16[1,1536,8960]{2,1,0:T(8,128)(2,1)} %all-gather.3.cloned.1.call-done, bf16[1,1,1,1536,8960]{4,3,2,1,0:T(8,128)(2,1)} %param.13, bf16[1,1,8192,1536]{3,2,1,0:T(8,128)(2,1)} %param.15), kind=kOutput, calls=%fused_computation.3.clone.clone.clone.clone.2 | convolution fusion | flops 230311854080 | bytes 227016704 | tf_op jit(solution)/shard_map/dot_general | solution.py:31
  1177.0 0.0 all-gather.5.cloned.1.call-done
  1177.0 252.1 %fusion.24 = f32[8192,1536]{1,0:T(8,128)} fusion(bf16[1,8960,1536]{2,1,0:T(8,128)(2,1)} %all-gather.5.cloned.1.call-done, bf16[1,1,1,8960,1536]{4,3,2,1,0:T(8,128)(2,1)} %param.14, f32[]{:T(128)S(6)} %convert_element_type.94, bf16[8192,8960]{0,1:T(8,128)(2,1)} %fusion.85), kind=kOutput, calls=%fused_computation.31 | convolution fusion | flops 225553416192 | bytes 252182528 | tf_op jit(solution)/shard_map/dot_general | solution.py:33
  1429.1 0.0 all-reduce.2.cloned.1.call-update
  1429.1 1094.5 %all-reduce.2.cloned.1.call-done = f32[8192,1536]{1,0:T(8,128)} async-done(((f32[8192,1536]{1,0:T(8,128)}), f32[8192,1536]{1,0:T(8,128)}) %all-reduce.2.cloned.1.call-update) | async-done | bytes 50331664 | tf_op jit(solution)/shard_map/psum | solution.py:34
  2523.6 32.7 %fusion.36 = bf16[1,1,8192,1536]{3,2,1,0:T(8,128)(2,1)} fusion(f32[8192,1536]{1,0:T(8,128)} %all-reduce.2.cloned.1.call-done, bf16[1,1,8192,1536]{3,2,1,0:T(8,128)(2,1)} %param.15, pred[]{:T(512)S(6)} %ge.3), kind=kLoop, calls=%fused_computation.37 | loop fusion | flops 50331648 | bytes 100663296 | tf_op jit(solution)/shard_map/broadcast_in_dim | solution.py:37
Async XLA Ops:
  7.2 334.5 %all-gather.3.cloned.1.call-start = ((), (), s32[]{:S(2)}) async-start(), calls=%async_computation | async-start | bytes 34406400 | tf_op jit(solution)/shard_map/all_gather | solution.py:23
  22.5 151.8 %collective-permute-start = (bf16[1,384,8960]{2,1,0:T(8,128)(2,1)S(1)}, bf16[1,384,8960]{2,1,0:T(8,128)(2,1)}, u32[]{:S(2)}, u32[]{:S(2)}) collective-permute-start(bf16[1,384,8960]{2,1,0:T(8,128)(2,1)S(1)} %get-tuple-element.5), channel_id=1, source_target_pairs={{0,4},{1,5},{2,6},{3,7}} | collective-permute-start | bytes 20643848 | tf_op jit(solution)/shard_map/ppermute | solution.py:21
  174.3 1002.7 %all-gather.5.cloned.1.call-start = ((), (), s32[]{:S(2)}) async-start(), calls=%async_computation.1 | async-start | bytes 34406400 | tf_op jit(solution)/shard_map/all_gather | solution.py:24
  190.6 151.0 %collective-permute-start.1 = (bf16[1,8960,384]{2,1,0:T(8,128)(2,1)}, bf16[1,8960,384]{2,1,0:T(8,128)(2,1)}, u32[]{:S(2)}, u32[]{:S(2)}) collective-permute-start(bf16[1,8960,384]{2,1,0:T(8,128)(2,1)} %get-tuple-element.3), channel_id=1, source_target_pairs={{0,4},{1,5},{2,6},{3,7}} | collective-permute-start | bytes 20643848 | tf_op jit(solution)/shard_map/ppermute | solution.py:22
  341.6 2182.0 %all-reduce.2.cloned.1.call-start = ((), (), s32[]{:S(2)}) async-start(), calls=%async_computation.2 | async-start | bytes 100663296 | tf_op jit(solution)/shard_map/psum | solution.py:34
Sparse Core Ops, SparseCore 0:
  174.5 166.8 all-gather.2
  342.9 165.4 all-gather.4
  1429.2 1094.3 all-reduce.1
where the time goes:
time: 2560 us
  waiting for transfers between devices  1390 us (54%)
  matrix products  1090 us (43%)
  other arithmetic  63.6 us (2%)
    psum x1, waiting for transfers between devices, local_step(): tp_total = lax.psum(part_sum * gen_mask, 'side')  1090 us
    dot_general x1, matrix products, local_step(): jnp.dot(hidden, gen_up[layer_idx], preferred_element_type=jnp.float32)  835 us
    dot_general x1, matrix products, local_step(): jnp.dot(act_val, gen_down[layer_idx], preferred_element_type=jnp.float32)  252 us
    ppermute x1, waiting for transfers between devices, local_step(): recv_up = lax.ppermute(delta_up, 'side', send_pairs)  150 us
    ppermute x1, waiting for transfers between devices, local_step(): recv_down = lax.ppermute(delta_down, 'side', send_pairs)  150 us
  transfers between devices with their start and end apart: 5, of which 3 were waited for; matrix products, arithmetic and copies ran while one was open for 33% of the time, Pallas kernels for 0%

commit v1 on v0

v1 whole, which is shorter than its diff:
```python
import jax
import jax.numpy as jnp
from jax import lax
from jax.experimental import pallas as pl
from jax.experimental.pallas import tpu as pltpu
from jax.sharding import PartitionSpec as P

MESH = pl.DeviceIdType.MESH
BF = jnp.bfloat16
F32 = jnp.float32

SMALL, LARGE = 256, 512
N_SMALL = 5
TILE = 1024
TILE_T = 256
VMEM_BYTES = 67043328


def gelu_bf16(v):
    return (0.5 * v * (1.0 + lax.erf(v * 0.7071067811865476))).astype(BF)


def dot(a, b):
    return jnp.dot(a, b, preferred_element_type=F32)


def make_step(D, F, B, reps):
    S = D // reps
    n_large = (F - N_SMALL * SMALL) // LARGE
    assert N_SMALL * SMALL + n_large * LARGE == F
    NCH = N_SMALL + n_large
    base_small = n_large * LARGE
    n_tok_t = TILE
    n_tok_g = B - n_tok_t
    NT = n_tok_g // TILE
    NTT = n_tok_t // TILE_T
    LAST = NCH - 1

    def piece_off(k, fc):
        if fc == SMALL:
            return pl.multiple_of(base_small + k * SMALL, SMALL)
        return pl.multiple_of((k - N_SMALL) * LARGE, LARGE)

    def sized(k, fn):
        if isinstance(k, int):
            if 0 <= k < NCH:
                fn(k, SMALL if k < N_SMALL else LARGE)
            return

        @pl.when(jnp.logical_and(k >= 0, k < N_SMALL))
        def _():
            fn(k, SMALL)

        @pl.when(jnp.logical_and(k >= N_SMALL, k < NCH))
        def _():
            fn(k, LARGE)

    def kern(lr, w_up, w_dn, g_up, g_dn, old_up, old_dn, x,
             q_up, q_dn, pay_up, pay_dn, wg_up, wg_dn, xr, ys, yr, pout,
             p, xb, wub, wdb, sq_up, sq_dn, so_up, so_dn,
             y_s, y_r, x_s, x_r, s_s, s_r, f_s, f_r, xt_s, xt_r, yt_s, yt_r,
             la, lb, lw, lx, lp, l0):
        side = lax.axis_index("side")
        r = lax.axis_index("rep")
        is_gen = side == 1
        peer = (1 - side, r)
        rx = lax.rem(r + 2, 4)
        rs = r + 1 - 2 * lax.rem(r, 2)
        xn = (side, rx)
        sib = (side, rs)

        barrier = pltpu.get_barrier_semaphore()
        for dev in (peer, xn, sib):
            pl.semaphore_signal(barrier, inc=1, device_id=dev, device_id_type=MESH)
        pl.semaphore_wait(barrier, 3)

        def rows(i):
            return pl.ds(pl.multiple_of(i * S, 128), S)

        def local(src, dst, sem):
            return pltpu.make_async_copy(src, dst, sem)

        def remote(src, dst, ss, rs_, dev):
            return pltpu.make_async_remote_copy(
                src_ref=src, dst_ref=dst, send_sem=ss, recv_sem=rs_,
                device_id=dev, device_id_type=MESH)

        def y_copies(k, fc, srcs):
            f = pl.ds(piece_off(k, fc), fc)
            a, b = srcs(f)
            return (remote(a, q_up.at[:, f], y_s.at[k, 0], y_r.at[k, 0], peer),
                    remote(b, q_dn.at[f, :], y_s.at[k, 1], y_r.at[k, 1], peer))

        def gen_src(f):
            return old_up.at[rows(r), f], old_dn.at[f, rows(r)]

        def trn_src(f):
            return pay_up.at[:, f], pay_dn.at[f, :]

        def x_copies(k, fc):
            f = pl.ds(piece_off(k, fc), fc)
            a, b = wg_up.at[rows(r), f], wg_dn.at[f, rows(r)]
            return (remote(a, a, x_s.at[k, 0], x_r.at[k, 0], xn),
                    remote(b, b, x_s.at[k, 1], x_r.at[k, 1], xn))

        def s_copies(k, fc):
            f = pl.ds(piece_off(k, fc), fc)
            a, b = wg_up.at[rows(r), f], wg_dn.at[f, rows(r)]
            return (remote(a, a, s_s.at[k, 0], s_r.at[k, 0], sib),
                    remote(b, b, s_s.at[k, 1], s_r.at[k, 1], sib))

        def f_copies(k, fc):
            f = pl.ds(piece_off(k, fc), fc)
            a, b = wg_up.at[rows(rx), f], wg_dn.at[f, rows(rx)]
            return (remote(a, a, f_s.at[k, 0], f_r.at[k, 0], sib),
                    remote(b, b, f_s.at[k, 1], f_r.at[k, 1], sib))

        def a_copies(k, fc, srcs):
            f = pl.ds(piece_off(k, fc), fc)
            a, b = srcs(f)
            return (local(q_up.at[:, f], sq_up.at[:, pl.ds(0, fc)], la.at[0]),
                    local(q_dn.at[f, :], sq_dn.at[pl.ds(0, fc), :], la.at[1]),
                    local(a, so_up.at[:, pl.ds(0, fc)], la.at[2]),
                    local(b, so_dn.at[pl.ds(0, fc), :], la.at[3]))

        def b_copies(k, fc):
            f = pl.ds(piece_off(k, fc), fc)
            return (local(so_up.at[:, pl.ds(0, fc)], wg_up.at[rows(r), f], lb.at[0]),
                    local(so_dn.at[pl.ds(0, fc), :], wg_dn.at[f, rows(r)], lb.at[1]))

        def step_a(srcs):
            def fn(k, fc):
                for c in y_copies(k, fc, srcs):
                    c.wait_recv()
                for c in a_copies(k, fc, srcs):
                    c.start()
            return fn

        def step_b(srcs):
            def fn(k, fc):
                for c in a_copies(k, fc, srcs):
                    c.wait()
                so_up[:, :fc] = (so_up[:, :fc].astype(F32) + sq_up[:, :fc].astype(F32)).astype(BF)
                so_dn[:fc, :] = (so_dn[:fc, :].astype(F32) + sq_dn[:fc, :].astype(F32)).astype(BF)
                for c in b_copies(k, fc):
                    c.start()
            return fn

        def step_c(k, fc):
            for c in b_copies(k, fc):
                c.wait()
            for c in x_copies(k, fc):
                c.start()
            for c in s_copies(k, fc):
                c.start()

        def step_d(k, fc):
            for c in x_copies(k, fc):
                c.wait_recv()
            for c in f_copies(k, fc):
                c.start()

        def arrive(k, fc):
            for c in s_copies(k, fc):
                c.wait_recv()
            for c in f_copies(k, fc):
                c.wait_recv()

        def w_copies(k, fc, slot):
            f = pl.ds(piece_off(k, fc), fc)
            return (local(wg_up.at[:, f], wub.at[slot, :, pl.ds(0, fc)], lw.at[slot, 0]),
                    local(wg_dn.at[f, :], wdb.at[slot, pl.ds(0, fc), :], lw.at[slot, 1]))

        def w_start(k, fc, slot):
            for c in w_copies(k, fc, slot):
                c.start()

        def w_wait(k, fc, slot):
            for c in w_copies(k, fc, slot):
                c.wait()

        def xt_copy(i):
            return remote(x.at[pl.ds(n_tok_g + i * TILE_T, TILE_T)], xr.at[pl.ds(i * TILE_T, TILE_T)],
                          xt_s.at[i], xt_r.at[i], peer)

        def yt_copy(i):
            return remote(ys.at[pl.ds(i * TILE_T, TILE_T)], yr.at[pl.ds(i * TILE_T, TILE_T)],
                          yt_s.at[i], yt_r.at[i], peer)

        def drain(srcs):
            def fn(k, fc):
                for cs in (y_copies(k, fc, srcs), x_copies(k, fc), s_copies(k, fc), f_copies(k, fc)):
                    for c in cs:
                        c.wait_send()

            @pl.loop(0, NCH)
            def _(k):
                sized(k, fn)

        @pl.when(is_gen)
        def _():
            for k in range(NCH):
                for c in y_copies(k, SMALL if k < N_SMALL else LARGE, gen_src):
                    c.start()
            for i in range(NTT):
                xt_copy(i).start()

            def x_load(t, slot):
                return local(x.at[pl.ds(pl.multiple_of(t * TILE, TILE), TILE)], xb.at[slot], lx.at[slot])

            def p_out(t):
                d = pl.ds(pl.multiple_of(t * TILE, TILE), TILE)
                return local(p.at[d], pout.at[d], lp.at[t])

            x_load(0, 0).start()

            @pl.loop(0, n_tok_g // 256)
            def _(i):
                p[pl.ds(pl.multiple_of(i * 256, 256), 256)] = jnp.zeros((256, D), F32)

            A, Bs = step_a(gen_src), step_b(gen_src)
            for k in range(2):
                sized(k, A)
                sized(k, Bs)
                sized(k, step_c)
            sized(0, step_d)
            arrive(0, SMALL)
            w_start(0, SMALL, 0)

            def tile_math(t, xs, s, fc):
                h = TILE // 2
                base = pl.multiple_of(t * TILE, TILE)
                pre_a = dot(xb[xs, :h], wub[s, :, :fc])
                u_a = gelu_bf16(pre_a)
                pre_b = dot(xb[xs, h:], wub[s, :, :fc])
                p[pl.ds(base, h)] += dot(u_a, wdb[s, :fc, :])
                u_b = gelu_bf16(pre_b)
                p[pl.ds(base + h, h)] += dot(u_b, wdb[s, :fc, :])

            def chunk(c, fc):
                s = lax.rem(c, 2)
                w_wait(c, fc, s)

                @pl.loop(0, NT)
                def _(t):
                    i = c * NT + t
                    xs = lax.rem(i, 2)
                    x_load(t, xs).wait()
                    x_load(lax.rem(t + 1, NT), 1 - xs).start()

                    @pl.when(t == 2)
                    def _():
                        sized(c + 2, A)

                    @pl.when(t == 3)
                    def _():
                        sized(c + 2, Bs)
                        sized(c + 1, step_d)

                    @pl.when(t == 4)
                    def _():
                        sized(c + 2, step_c)

                    @pl.when(t == 5)
                    def _():
                        def load_next(k, fck):
                            arrive(k, fck)

                            @pl.when(k < LAST)
                            def _():
                                w_start(k, fck, 1 - s)
                        sized(c + 1, load_next)

                    tile_math(t, xs, s, fc)

                    @pl.when(c == LAST - 1)
                    def _():
                        p_out(t).start()

            @pl.loop(0, N_SMALL)
            def _(c):
                chunk(c, SMALL)

            @pl.loop(N_SMALL, LAST)
            def _(c):
                chunk(c, LARGE)

            x_load(0, (LAST * NT) % 2).wait()
            for t in range(NT):
                p_out(t).wait()
            for i in range(NTT):
                yt_copy(i).wait_recv()
            drain(gen_src)
            for i in range(NTT):
                xt_copy(i).wait_send()

        @pl.when(jnp.logical_not(is_gen))
        def _():
            rate = lr[0]

            def u_load(k, fc):
                f = pl.ds(piece_off(k, fc), fc)
                return (local(w_up.at[:, f], p.at[pl.ds(0, S), pl.ds(0, fc)], l0.at[0]),
                        local(g_up.at[:, f], p.at[pl.ds(S, S), pl.ds(0, fc)], l0.at[1]),
                        local(w_dn.at[f, :], p.at[pl.ds(2 * S, fc), pl.ds(0, S)], l0.at[2]),
                        local(g_dn.at[f, :], p.at[pl.ds(2 * S + LARGE, fc), pl.ds(0, S)], l0.at[3]))

            def u_store(k, fc):
                f = pl.ds(piece_off(k, fc), fc)
                return (local(wub.at[0, pl.ds(0, S), pl.ds(0, fc)], pay_up.at[:, f], l0.at[4]),
                        local(wdb.at[0, pl.ds(0, fc), pl.ds(0, S)], pay_dn.at[f, :], l0.at[5]))

            def u_start(k, fc):
                for c in u_load(k, fc):
                    c.start()

            def u_math(k, fc):
                for c in u_load(k, fc):
                    c.wait()
                w = p[:S, :fc]
                new = w - rate * p[S:2 * S, :fc]
                wub[0, :S, :fc] = (new - w).astype(BF)
                w = p[2 * S:2 * S + fc, :S]
                new = w - rate * p[2 * S + LARGE:2 * S + LARGE + fc, :S]
                wdb[0, :fc, :S] = (new - w).astype(BF)
                for c in u_store(k, fc):
                    c.start()

            def u_send(k, fc):
                for c in u_store(k, fc):
                    c.wait()
                for c in y_copies(k, fc, trn_src):
                    c.start()

            for k in range(2):
                sized(k, u_start)
                sized(k, u_math)
                sized(k, u_send)
            A, Bs = step_a(trn_src), step_b(trn_src)

            @pl.loop(0, NCH)
            def _(k):
                sized(k + 2, u_start)
                sized(k, A)
                sized(k + 2, u_math)
                sized(k, Bs)
                sized(k + 2, u_send)
                sized(k, step_c)
                sized(k - 1, step_d)

            sized(NCH - 1, step_d)

            def x_load(i):
                return local(xr.at[pl.ds(i * TILE_T, TILE_T)], xb.at[0, pl.ds(0, TILE_T)], lx.at[0])

            def y_out(i):
                return local(xb.at[1, pl.ds(0, TILE_T)], ys.at[pl.ds(i * TILE_T, TILE_T)], lx.at[1])

            arrive(0, SMALL)
            w_start(0, SMALL, 0)

            @pl.loop(0, NTT)
            def _(i):
                xt_copy(i).wait_recv()
                x_load(i).start()
                p[:TILE_T] = jnp.zeros((TILE_T, D), F32)
                x_load(i).wait()

                def piece(k, fc):
                    s = lax.rem(k, 2)
                    w_wait(k, fc, s)

                    def nxt(kn, fcn):
                        @pl.when(i == 0)
                        def _():
                            arrive(kn, fcn)
                        w_start(kn, fcn, 1 - s)
                    sized(k + 1, nxt)

                    @pl.when(jnp.logical_and(k == LAST, i < NTT - 1))
                    def _():
                        w_start(0, SMALL, 1 - s)

                    if fc == SMALL:
                        u = gelu_bf16(dot(xb[0, :TILE_T], wub[s, :, :fc]))
                        p[:TILE_T] += dot(u, wdb[s, :fc, :])
                    else:
                        h = fc // 2
                        pre_a = dot(xb[0, :TILE_T], wub[s, :, :h])
                        u_a = gelu_bf16(pre_a)
                        pre_b = dot(xb[0, :TILE_T], wub[s, :, h:])
                        acc = dot(u_a, wdb[s, :h, :])
                        u_b = gelu_bf16(pre_b)
                        p[:TILE_T] += acc + dot(u_b, wdb[s, h:, :])

                @pl.loop(0, N_SMALL)
                def _(k):
                    piece(k, SMALL)

                @pl.loop(N_SMALL, NCH)
                def _(k):
                    piece(k, LARGE)

                xb[1, :TILE_T] = (xb[0, :TILE_T].astype(F32) + p[:TILE_T]).astype(BF)
                y_out(i).start()
                y_out(i).wait()
                yt_copy(i).start()

            drain(trn_src)
            for i in range(NTT):
                yt_copy(i).wait_send()

    def first(lr, w_up, w_dn, g_up, g_dn, old_up, old_dn, x):
        sds = jax.ShapeDtypeStruct
        outs = (sds((S, F), BF), sds((F, S), BF), sds((S, F), BF), sds((F, S), BF),
                sds((D, F), BF), sds((F, D), BF),
                sds((n_tok_t, D), BF), sds((n_tok_t, D), BF), sds((n_tok_t, D), BF),
                sds((n_tok_g, D), F32))
        dma = pltpu.SemaphoreType.DMA
        anyspace = pl.BlockSpec(memory_space=pl.ANY)
        return pl.pallas_call(
            kern,
            out_shape=outs,
            in_specs=[pl.BlockSpec(memory_space=pltpu.SMEM)] + [anyspace] * 7,
            out_specs=[anyspace] * len(outs),
            scratch_shapes=[
                pltpu.VMEM((n_tok_g, D), F32),
                pltpu.VMEM((2, TILE, D), BF),
                pltpu.VMEM((2, D, LARGE), BF),
                pltpu.VMEM((2, LARGE, D), BF),
                pltpu.VMEM((S, LARGE), BF), pltpu.VMEM((LARGE, S), BF),
                pltpu.VMEM((S, LARGE), BF), pltpu.VMEM((LARGE, S), BF),
            ] + [dma((NCH, 2))] * 8 + [dma((NTT,))] * 4 + [
                dma((4,)), dma((2,)), dma((2, 2)), dma((2,)), dma((NT,)), dma((6,)),
            ],
            compiler_params=pltpu.CompilerParams(
                collective_id=0, has_side_effects=True, vmem_limit_bytes=VMEM_BYTES),
            name="sync_and_mlp",
        )(lr, w_up, w_dn, g_up, g_dn, old_up, old_dn, x)

    def kern2(x_ref, p_ref, wu_ref, wd_ref, yr_ref, y_ref):
        t = pl.program_id(0)
        is_gen = lax.axis_index("side") == 1

        @pl.when(jnp.logical_not(is_gen))
        def _():
            y_ref[...] = jnp.zeros_like(y_ref)

        @pl.when(jnp.logical_and(is_gen, t == NT))
        def _():
            y_ref[...] = yr_ref[...]

        @pl.when(jnp.logical_and(is_gen, t < NT))
        def _():
            h = TILE // 2
            pre_a = dot(x_ref[:h], wu_ref[...])
            u_a = gelu_bf16(pre_a)
            pre_b = dot(x_ref[h:], wu_ref[...])
            y_ref[:h] = (x_ref[:h].astype(F32) + (p_ref[:h] + dot(u_a, wd_ref[...]))).astype(BF)
            u_b = gelu_bf16(pre_b)
            y_ref[h:] = (x_ref[h:].astype(F32) + (p_ref[h:] + dot(u_b, wd_ref[...]))).astype(BF)

    def second(x, pout, wg_up, wg_dn, yr):
        jl = n_large - 1
        return pl.pallas_call(
            kern2,
            out_shape=jax.ShapeDtypeStruct((B, D), BF),
            grid=(NT + 1,),
            in_specs=[
                pl.BlockSpec((TILE, D), lambda t: (t, 0)),
                pl.BlockSpec((TILE, D), lambda t: (jnp.minimum(t, NT - 1), 0)),
                pl.BlockSpec((D, LARGE), lambda t: (0, jl)),
                pl.BlockSpec((LARGE, D), lambda t: (jl, 0)),
                pl.BlockSpec((n_tok_t, D), lambda t: (0, 0)),
            ],
            out_specs=pl.BlockSpec((TILE, D), lambda t: (t, 0)),
            compiler_params=pltpu.CompilerParams(vmem_limit_bytes=VMEM_BYTES),
            name="last_piece",
        )(x, pout, wg_up, wg_dn, yr)

    return first, second


def solution(mesh):
    reps = mesh.shape["rep"]
    up_spec = P("side", None, "rep", None)
    down_spec = P("side", None, None, "rep")
    copy_spec = P("side", "rep", None, None, None)
    token_spec = P("side", "rep", None, None)

    def local_step(w_up, w_down, g_up, g_down, learn_rate, old_up, old_down, prompts):
        B, D = prompts.shape[2:]
        F = w_up.shape[3]
        first, second = make_step(D, F, B, reps)
        x = prompts[0, 0]
        outs = first(learn_rate, w_up[0, 0], w_down[0, 0], g_up[0, 0], g_down[0, 0],
                     old_up[0, 0, 0], old_down[0, 0, 0], x)
        wg_up, wg_dn, yr, pout = outs[4], outs[5], outs[8], outs[9]
        y = second(x, pout, wg_up, wg_dn, yr)
        new_up = w_up - learn_rate[0] * g_up
        new_down = w_down - learn_rate[0] * g_down
        return new_up, new_down, y[None, None]

    return jax.shard_map(
        local_step,
        mesh=mesh,
        in_specs=(up_spec, down_spec, up_spec, down_spec, P(None), copy_spec, copy_spec, token_spec),
        out_specs=(up_spec, down_spec, token_spec),
        check_vma=False,
    )
```

time: 2560 us -> 559 us (0.22)
  waiting for transfers between devices: 1390 us -> 0 us
  matrix products: 1090 us -> 0 us
  Pallas kernels: 0 us -> 529 us
  other arithmetic: 63.6 us -> 20.8 us
    psum x1 -> x0, waiting for transfers between devices: 1090 us -> none  [local_step(): tp_total = lax.psum(part_sum * gen_mask, 'side')]
    dot_general x2 -> x0, matrix products: 1090 us -> none  [the longest x1 835 us: local_step(): jnp.dot(hidden, gen_up[layer_idx], preferred_element_type=jnp.float32)]
    pallas_call x0 -> x2, Pallas kernels: none -> 529 us  [the longest x1 489 us: first(): pl.pallas_call(kern, out_shape=outs, in_specs=[pl.BlockSpec(memory_space=...]
    ppermute x2 -> x0, waiting for transfers between devices: 300 us -> none  [the longest x1 150 us: local_step(): recv_up = lax.ppermute(delta_up, 'side', send_pairs)]
    broadcast_in_dim x1 -> x0, other arithmetic: 32.7 us -> none  [local_step(): return (new_up, new_down, y_local[None, None])]
    convert_element_type x2 -> x0, other arithmetic: 30.9 us -> none  [the longest x1 16.2 us: local_step(): delta_down = (new_down - w_down)[0].astype(jnp.bfloat16)]
  transfers between devices with their start and end apart: 5 -> 0, of which waited for: 3 -> 0; matrix products, arithmetic and copies ran while one was open for 33% -> 0% of each run, Pallas kernels for 0% -> 0%
where the time goes in v1:
time: 559 us; the launch traced here: 557 us
  Pallas kernels  529 us (95%)
  other arithmetic  20.8 us (4%)
  local copies, waits for them, and re-layouts  6.33 us (1%)
    pallas_call x1, Pallas kernels, first(): pl.pallas_call(kern, out_shape=outs, in_specs=[pl.BlockSpec(memory_space=...  489 us
    pallas_call x1, Pallas kernels, second(): pl.pallas_call(kern2, out_shape=jax.ShapeDtypeStruct((B, D), BF), grid=(N...  39.5 us
    sub x1, other arithmetic, local_step(): new_down = w_down - learn_rate[0] * g_down  15.4 us

profile of v1, /device:TPU:4, one launch (start us, length us, event | category | flops | bytes accessed | tf_op | source)
XLA Modules:
  0.0 557.3 jit_solution(12614999432584310317)
XLA Ops:
  1.3 489.3 %sync_and_mlp.1 = (bf16[384,8960]{1,0:T(8,128)(2,1)}, bf16[8960,384]{1,0:T(8,128)(2,1)}, bf16[384,8960]{1,0:T(8,128)(2,1)}, bf16[8960,384]{1,0:T(8,128)(2,1)}, b...) custom-call(f32[1]{0:T(128)} %copy.11.lr, ...), custom_call_target="tpu_custom_call" | custom-call | tf_op jit(solution)/shard_map/sync_and_mlp/pallas_call | solution.py:421
  490.6 39.5 %last_piece.1 = bf16[8192,1536]{1,0:T(8,128)(2,1)} custom-call(bf16[8192,1536]{1,0:T(8,128)(2,1)} %bitcast.12, f32[7168,1536]{1,0:T(8,128)} %get-tuple-element.7.p_ref, bf16[1536,8960]{1,0:T(8,128)(2,1)} %get-tuple-element.8.wu_ref, bf16[8960,1536]{1,0:T(8,128)(2,1)} %get-tuple-element.9.wd_ref, bf16[1024,1536]{1,0:T(8,128)(2,1)} %get-tuple-element.10.yr_ref), custom_call_target="tpu_custom_call" | custom-call | tf_op jit(solution)/shard_map/last_piece/pallas_call | solution.py:465
  530.1 0.0 copy-start
  530.1 0.0 copy-start.1
  530.1 15.4 %multiply_subtract_fusion = f32[1,1,8960,384]{3,2,1,0:T(8,128)} fusion(f32[1,1,8960,384]{3,2,1,0:T(8,128)} %param.9, f32[1,1,8960,384]{3,2,1,0:T(8,128)} %param.11, f32[]{:T(128)} %bitcast.10), kind=kLoop, calls=%fused_computation | loop fusion | flops 6881280 | bytes 41287684 | tf_op jit(solution)/shard_map/sub | solution.py:501
  545.5 2.4 copy-done
  547.9 3.9 copy-done.1
  551.8 5.5 multiply_subtract_fusion.1
Async XLA Ops:
  530.1 17.8 %copy-start = (f32[1,1,384,8960]{3,2,1,0:T(8,128)S(1)}, f32[1,1,384,8960]{3,2,1,0:T(8,128)}, u32[]{:S(2)}) copy-start(f32[1,1,384,8960]{3,2,1,0:T(8,128)} %param.8) | copy-start | bytes 41287684
  530.1 21.7 %copy-start.1 = (f32[1,1,384,8960]{3,2,1,0:T(8,128)S(1)}, f32[1,1,384,8960]{3,2,1,0:T(8,128)}, u32[]{:S(2)}) copy-start(f32[1,1,384,8960]{3,2,1,0:T(8,128)} %param.10) | copy-start | bytes 41287684

commit v2 on v1

--- a/solution.py
+++ b/solution.py
@@ -13,6 +13,9 @@
 N_SMALL = 5
 TILE = 1024
 TILE_T = 256
+LEAD_T = 5
+DEPTH = 4
+N_SECOND = 2
 VMEM_BYTES = 67043328
 
 
@@ -34,12 +37,12 @@
     n_tok_g = B - n_tok_t
     NT = n_tok_g // TILE
     NTT = n_tok_t // TILE_T
-    LAST = NCH - 1
+    N_FIRST = NCH - N_SECOND
 
     def piece_off(k, fc):
         if fc == SMALL:
             return pl.multiple_of(base_small + k * SMALL, SMALL)
-        return pl.multiple_of((k - N_SMALL) * LARGE, LARGE)
+        return pl.multiple_of((NCH - 1 - k) * LARGE, LARGE)
 
     def sized(k, fn):
         if isinstance(k, int):
@@ -57,7 +60,7 @@
 
     def kern(lr, w_up, w_dn, g_up, g_dn, old_up, old_dn, x,
              q_up, q_dn, pay_up, pay_dn, wg_up, wg_dn, xr, ys, yr, pout,
-             p, xb, wub, wdb, sq_up, sq_dn, so_up, so_dn,
+             sq_up, sq_dn, so_up, so_dn,
              y_s, y_r, x_s, x_r, s_s, s_r, f_s, f_r, xt_s, xt_r, yt_s, yt_r,
              la, lb, lw, lx, lp, l0):
         side = lax.axis_index("side")
@@ -166,18 +169,20 @@
             for c in f_copies(k, fc):
                 c.wait_recv()
 
-        def w_copies(k, fc, slot):
-            f = pl.ds(piece_off(k, fc), fc)
-            return (local(wg_up.at[:, f], wub.at[slot, :, pl.ds(0, fc)], lw.at[slot, 0]),
-                    local(wg_dn.at[f, :], wdb.at[slot, pl.ds(0, fc), :], lw.at[slot, 1]))
-
-        def w_start(k, fc, slot):
-            for c in w_copies(k, fc, slot):
-                c.start()
-
-        def w_wait(k, fc, slot):
-            for c in w_copies(k, fc, slot):
-                c.wait()
+        def w_stream(wub, wdb):
+            def copies(k, fc, slot):
+                f = pl.ds(piece_off(k, fc), fc)
+                return (local(wg_up.at[:, f], wub.at[slot, :, pl.ds(0, fc)], lw.at[slot, 0]),
+                        local(wg_dn.at[f, :], wdb.at[slot, pl.ds(0, fc), :], lw.at[slot, 1]))
+
+            def start(k, fc, slot):
+                for c in copies(k, fc, slot):
+                    c.start()
+
+            def wait(k, fc, slot):
+                for c in copies(k, fc, slot):
+                    c.wait()
+            return start, wait
 
         def xt_copy(i):
             return remote(x.at[pl.ds(n_tok_g + i * TILE_T, TILE_T)], xr.at[pl.ds(i * TILE_T, TILE_T)],
@@ -197,8 +202,8 @@
             def _(k):
                 sized(k, fn)
 
-        @pl.when(is_gen)
-        def _():
+        def generator(p, xb, wub, wdb):
+            w_start, w_wait = w_stream(wub, wdb)
             for k in range(NCH):
                 for c in y_copies(k, SMALL if k < N_SMALL else LARGE, gen_src):
                     c.start()
@@ -237,7 +242,7 @@
                 u_b = gelu_bf16(pre_b)
                 p[pl.ds(base + h, h)] += dot(u_b, wdb[s, :fc, :])
 
-            def chunk(c, fc):
+            def chunk(c, fc, sized):
                 s = lax.rem(c, 2)
                 w_wait(c, fc, s)
 
@@ -248,44 +253,50 @@
                     x_load(t, xs).wait()
                     x_load(lax.rem(t + 1, NT), 1 - xs).start()
 
+                    @pl.when(t == 0)
+                    def _():
+                        sized(c + 2, A)
+
+                    @pl.when(t == 1)
+                    def _():
+                        sized(c + 2, Bs)
+
                     @pl.when(t == 2)
                     def _():
-                        sized(c + 2, A)
-
-                    @pl.when(t == 3)
-                    def _():
-                        sized(c + 2, Bs)
+                        sized(c + 2, step_c)
+
+                    @pl.when(t == 4)
+                    def _():
                         sized(c + 1, step_d)
 
-                    @pl.when(t == 4)
-                    def _():
-                        sized(c + 2, step_c)
-
-                    @pl.when(t == 5)
+                    @pl.when(t == 6)
                     def _():
                         def load_next(k, fck):
                             arrive(k, fck)
 
-                            @pl.when(k < LAST)
+                            @pl.when(k < N_FIRST)
                             def _():
                                 w_start(k, fck, 1 - s)
                         sized(c + 1, load_next)
 
                     tile_math(t, xs, s, fc)
 
-                    @pl.when(c == LAST - 1)
+                    @pl.when(c == N_FIRST - 1)
                     def _():
                         p_out(t).start()
 
             @pl.loop(0, N_SMALL)
             def _(c):
-                chunk(c, SMALL)
-
-            @pl.loop(N_SMALL, LAST)
+                chunk(c, SMALL, sized)
+
+            @pl.loop(N_SMALL, N_FIRST)
             def _(c):
-                chunk(c, LARGE)
-
-            x_load(0, (LAST * NT) % 2).wait()
+                chunk(c, LARGE, lambda k, fn: fn(k, LARGE))
+
+            x_load(0, (N_FIRST * NT) % 2).wait()
+            for k in range(N_FIRST + 1, NCH):
+                sized(k, step_d)
+                sized(k, arrive)
             for t in range(NT):
                 p_out(t).wait()
             for i in range(NTT):
@@ -294,16 +305,16 @@
             for i in range(NTT):
                 xt_copy(i).wait_send()
 
-        @pl.when(jnp.logical_not(is_gen))
-        def _():
+        def trainer(p, st, xb, wub, wdb):
+            w_start, w_wait = w_stream(wub, wdb)
             rate = lr[0]
 
             def u_load(k, fc):
                 f = pl.ds(piece_off(k, fc), fc)
-                return (local(w_up.at[:, f], p.at[pl.ds(0, S), pl.ds(0, fc)], l0.at[0]),
-                        local(g_up.at[:, f], p.at[pl.ds(S, S), pl.ds(0, fc)], l0.at[1]),
-                        local(w_dn.at[f, :], p.at[pl.ds(2 * S, fc), pl.ds(0, S)], l0.at[2]),
-                        local(g_dn.at[f, :], p.at[pl.ds(2 * S + LARGE, fc), pl.ds(0, S)], l0.at[3]))
+                return (local(w_up.at[:, f], st.at[pl.ds(0, S), pl.ds(0, fc)], l0.at[0]),
+                        local(g_up.at[:, f], st.at[pl.ds(S, S), pl.ds(0, fc)], l0.at[1]),
+                        local(w_dn.at[f, :], st.at[pl.ds(2 * S, fc), pl.ds(0, S)], l0.at[2]),
+                        local(g_dn.at[f, :], st.at[pl.ds(2 * S + LARGE, fc), pl.ds(0, S)], l0.at[3]))
 
             def u_store(k, fc):
                 f = pl.ds(piece_off(k, fc), fc)
@@ -317,11 +328,11 @@
             def u_math(k, fc):
                 for c in u_load(k, fc):
                     c.wait()
-                w = p[:S, :fc]
-                new = w - rate * p[S:2 * S, :fc]
+                w = st[:S, :fc]
+                new = w - rate * st[S:2 * S, :fc]
                 wub[0, :S, :fc] = (new - w).astype(BF)
-                w = p[2 * S:2 * S + fc, :S]
-                new = w - rate * p[2 * S + LARGE:2 * S + LARGE + fc, :S]
+                w = st[2 * S:2 * S + fc, :S]
+                new = w - rate * st[2 * S + LARGE:2 * S + LARGE + fc, :S]
                 wdb[0, :fc, :S] = (new - w).astype(BF)
                 for c in u_store(k, fc):
                     c.start()
@@ -332,7 +343,7 @@
                 for c in y_copies(k, fc, trn_src):
                     c.start()
 
-            for k in range(2):
+            for k in range(LEAD_T):
                 sized(k, u_start)
                 sized(k, u_math)
                 sized(k, u_send)
@@ -340,58 +351,50 @@
 
             @pl.loop(0, NCH)
             def _(k):
-                sized(k + 2, u_start)
+                sized(k + LEAD_T, u_start)
                 sized(k, A)
-                sized(k + 2, u_math)
+                sized(k + LEAD_T, u_math)
                 sized(k, Bs)
-                sized(k + 2, u_send)
+                sized(k + LEAD_T, u_send)
                 sized(k, step_c)
                 sized(k - 1, step_d)
 
             sized(NCH - 1, step_d)
 
             def x_load(i):
-                return local(xr.at[pl.ds(i * TILE_T, TILE_T)], xb.at[0, pl.ds(0, TILE_T)], lx.at[0])
+                return local(xr.at[pl.ds(i * TILE_T, TILE_T)], xb.at[0], lx.at[0])
 
             def y_out(i):
-                return local(xb.at[1, pl.ds(0, TILE_T)], ys.at[pl.ds(i * TILE_T, TILE_T)], lx.at[1])
-
-            arrive(0, SMALL)
-            w_start(0, SMALL, 0)
+                return local(xb.at[1], ys.at[pl.ds(i * TILE_T, TILE_T)], lx.at[1])
+
+            for k in range(DEPTH - 1):
+                arrive(k, SMALL)
+                w_start(k, SMALL, k)
 
             @pl.loop(0, NTT)
             def _(i):
                 xt_copy(i).wait_recv()
                 x_load(i).start()
-                p[:TILE_T] = jnp.zeros((TILE_T, D), F32)
+                p[...] = jnp.zeros((TILE_T, D), F32)
                 x_load(i).wait()
 
                 def piece(k, fc):
-                    s = lax.rem(k, 2)
+                    s = lax.rem(k, DEPTH)
                     w_wait(k, fc, s)
+                    ahead = lax.rem(k + DEPTH - 1, DEPTH)
 
                     def nxt(kn, fcn):
                         @pl.when(i == 0)
                         def _():
                             arrive(kn, fcn)
-                        w_start(kn, fcn, 1 - s)
-                    sized(k + 1, nxt)
-
-                    @pl.when(jnp.logical_and(k == LAST, i < NTT - 1))
-                    def _():
-                        w_start(0, SMALL, 1 - s)
-
-                    if fc == SMALL:
-                        u = gelu_bf16(dot(xb[0, :TILE_T], wub[s, :, :fc]))
-                        p[:TILE_T] += dot(u, wdb[s, :fc, :])
-                    else:
-                        h = fc // 2
-                        pre_a = dot(xb[0, :TILE_T], wub[s, :, :h])
-                        u_a = gelu_bf16(pre_a)
-                        pre_b = dot(xb[0, :TILE_T], wub[s, :, h:])
-                        acc = dot(u_a, wdb[s, :h, :])
-                        u_b = gelu_bf16(pre_b)
-                        p[:TILE_T] += acc + dot(u_b, wdb[s, h:, :])
+                        w_start(kn, fcn, ahead)
+                    sized(k + DEPTH - 1, nxt)
+
+                    @pl.when(jnp.logical_and(k + DEPTH - 1 >= NCH, i < NTT - 1))
+                    def _():
+                        w_start(k + DEPTH - 1 - NCH, SMALL, ahead)
+
+                    trainer_math(p, xb, wub, wdb, s, fc)
 
                 @pl.loop(0, N_SMALL)
                 def _(k):
@@ -401,7 +404,7 @@
                 def _(k):
                     piece(k, LARGE)
 
-                xb[1, :TILE_T] = (xb[0, :TILE_T].astype(F32) + p[:TILE_T]).astype(BF)
+                xb[1] = (xb[0].astype(F32) + p[...]).astype(BF)
                 y_out(i).start()
                 y_out(i).wait()
                 yt_copy(i).start()
@@ -409,6 +412,26 @@
             drain(trn_src)
             for i in range(NTT):
                 yt_copy(i).wait_send()
+
+        @pl.when(is_gen)
+        def _():
+            pl.run_scoped(generator, pltpu.VMEM((n_tok_g, D), F32), pltpu.VMEM((2, TILE, D), BF),
+                          pltpu.VMEM((2, D, LARGE), BF), pltpu.VMEM((2, LARGE, D), BF))
+
+        @pl.when(jnp.logical_not(is_gen))
+        def _():
+            pl.run_scoped(trainer, pltpu.VMEM((TILE_T, D), F32), pltpu.VMEM((2 * S + 2 * LARGE, LARGE), F32),
+                          pltpu.VMEM((2, TILE_T, D), BF),
+                          pltpu.VMEM((DEPTH, D, LARGE), BF), pltpu.VMEM((DEPTH, LARGE, D), BF))
+
+    def trainer_math(p, xb, wub, wdb, s, fc):
+        h = TILE_T // 2
+        pre_a = dot(xb[0, :h], wub[s, :, :fc])
+        u_a = gelu_bf16(pre_a)
+        pre_b = dot(xb[0, h:], wub[s, :, :fc])
+        p[:h] += dot(u_a, wdb[s, :fc, :])
+        u_b = gelu_bf16(pre_b)
+        p[h:] += dot(u_b, wdb[s, :fc, :])
 
     def first(lr, w_up, w_dn, g_up, g_dn, old_up, old_dn, x):
         sds = jax.ShapeDtypeStruct
@@ -424,33 +447,64 @@
             in_specs=[pl.BlockSpec(memory_space=pltpu.SMEM)] + [anyspace] * 7,
             out_specs=[anyspace] * len(outs),
             scratch_shapes=[
-                pltpu.VMEM((n_tok_g, D), F32),
-                pltpu.VMEM((2, TILE, D), BF),
-                pltpu.VMEM((2, D, LARGE), BF),
-                pltpu.VMEM((2, LARGE, D), BF),
                 pltpu.VMEM((S, LARGE), BF), pltpu.VMEM((LARGE, S), BF),
                 pltpu.VMEM((S, LARGE), BF), pltpu.VMEM((LARGE, S), BF),
             ] + [dma((NCH, 2))] * 8 + [dma((NTT,))] * 4 + [
-                dma((4,)), dma((2,)), dma((2, 2)), dma((2,)), dma((NT,)), dma((6,)),
+                dma((4,)), dma((2,)), dma((DEPTH, 2)), dma((2,)), dma((NT,)), dma((6,)),
             ],
             compiler_params=pltpu.CompilerParams(
                 collective_id=0, has_side_effects=True, vmem_limit_bytes=VMEM_BYTES),
             name="sync_and_mlp",
         )(lr, w_up, w_dn, g_up, g_dn, old_up, old_dn, x)
 
-    def kern2(x_ref, p_ref, wu_ref, wd_ref, yr_ref, y_ref):
+    bu, bd = S // (NT + 1), F // (NT + 1)
+
+    def kern2(role, lr, x_ref, p_ref, wu_ref, wd_ref, yr_ref, w_up, g_up, w_dn, g_dn,
+              y_ref, new_up, new_dn, uw, ug, dw, dg, sem):
         t = pl.program_id(0)
         is_gen = lax.axis_index("side") == 1
 
+        def in_copies():
+            u, d = pl.ds(t * bu, bu), pl.ds(t * bd, bd)
+            return (pltpu.make_async_copy(w_up.at[u], uw, sem.at[0]),
+                    pltpu.make_async_copy(g_up.at[u], ug, sem.at[1]),
+                    pltpu.make_async_copy(w_dn.at[d], dw, sem.at[2]),
+                    pltpu.make_async_copy(g_dn.at[d], dg, sem.at[3]))
+
+        def out_copies():
+            u, d = pl.ds(t * bu, bu), pl.ds(t * bd, bd)
+            return (pltpu.make_async_copy(uw, new_up.at[u], sem.at[4]),
+                    pltpu.make_async_copy(dw, new_dn.at[d], sem.at[5]))
+
         @pl.when(jnp.logical_not(is_gen))
         def _():
+            for c in in_copies():
+                c.start()
             y_ref[...] = jnp.zeros_like(y_ref)
-
-        @pl.when(jnp.logical_and(is_gen, t == NT))
+            for c in in_copies():
+                c.wait()
+            uw[...] = uw[...] - lr[0] * ug[...]
+            dw[...] = dw[...] - lr[0] * dg[...]
+            for c in out_copies():
+                c.start()
+            for c in out_copies():
+                c.wait()
+
+        @pl.when(is_gen)
+        def _():
+            @pl.when(t == 0)
+            def _():
+                uw[...] = jnp.zeros_like(uw)
+                dw[...] = jnp.zeros_like(dw)
+
+            for c in out_copies():
+                c.start()
+
+        @pl.when(is_gen & (t == NT))
         def _():
             y_ref[...] = yr_ref[...]
 
-        @pl.when(jnp.logical_and(is_gen, t < NT))
+        @pl.when(is_gen & (t < NT))
         def _():
             h = TILE // 2
             pre_a = dot(x_ref[:h], wu_ref[...])
@@ -460,23 +514,41 @@
             u_b = gelu_bf16(pre_b)
             y_ref[h:] = (x_ref[h:].astype(F32) + (p_ref[h:] + dot(u_b, wd_ref[...]))).astype(BF)
 
-    def second(x, pout, wg_up, wg_dn, yr):
-        jl = n_large - 1
+        @pl.when(is_gen)
+        def _():
+            for c in out_copies():
+                c.wait()
+
+    def second(role, lr, x, pout, wg_up, wg_dn, yr, w_up, g_up, w_dn, g_dn):
+        fs = N_SECOND * LARGE
+        assert bu * (NT + 1) == S and bd * (NT + 1) == F and bu % 8 == 0 and bd % 8 == 0
+        once = pl.Buffered(1)
+        anyspace = pl.BlockSpec(memory_space=pl.ANY)
         return pl.pallas_call(
             kern2,
-            out_shape=jax.ShapeDtypeStruct((B, D), BF),
-            grid=(NT + 1,),
-            in_specs=[
-                pl.BlockSpec((TILE, D), lambda t: (t, 0)),
-                pl.BlockSpec((TILE, D), lambda t: (jnp.minimum(t, NT - 1), 0)),
-                pl.BlockSpec((D, LARGE), lambda t: (0, jl)),
-                pl.BlockSpec((LARGE, D), lambda t: (jl, 0)),
-                pl.BlockSpec((n_tok_t, D), lambda t: (0, 0)),
-            ],
-            out_specs=pl.BlockSpec((TILE, D), lambda t: (t, 0)),
+            out_shape=(jax.ShapeDtypeStruct((B, D), BF),
+                       jax.ShapeDtypeStruct((S, F), F32), jax.ShapeDtypeStruct((F, S), F32)),
+            grid_spec=pltpu.PrefetchScalarGridSpec(
+                num_scalar_prefetch=1,
+                grid=(NT + 1,),
+                in_specs=[
+                    pl.BlockSpec(memory_space=pltpu.SMEM),
+                    pl.BlockSpec((TILE, D), lambda t, role: (jnp.minimum(t, NT - 1) * role[0], 0)),
+                    pl.BlockSpec((TILE, D), lambda t, role: (jnp.minimum(t, NT - 1) * role[0], 0)),
+                    pl.BlockSpec((D, fs), lambda t, role: (0, 0), pipeline_mode=once),
+                    pl.BlockSpec((fs, D), lambda t, role: (0, 0), pipeline_mode=once),
+                    pl.BlockSpec((n_tok_t, D), lambda t, role: (0, 0), pipeline_mode=once),
+                ] + [anyspace] * 4,
+                out_specs=[pl.BlockSpec((TILE, D), lambda t, role: (t, 0)), anyspace, anyspace],
+                scratch_shapes=[
+                    pltpu.VMEM((bu, F), F32), pltpu.VMEM((bu, F), F32),
+                    pltpu.VMEM((bd, S), F32), pltpu.VMEM((bd, S), F32),
+                    pltpu.SemaphoreType.DMA((6,)),
+                ],
+            ),
             compiler_params=pltpu.CompilerParams(vmem_limit_bytes=VMEM_BYTES),
-            name="last_piece",
-        )(x, pout, wg_up, wg_dn, yr)
+            name="last_pieces",
+        )(role, lr, x, pout, wg_up, wg_dn, yr, w_up, g_up, w_dn, g_dn)
 
     return first, second
 
@@ -496,10 +568,10 @@
         outs = first(learn_rate, w_up[0, 0], w_down[0, 0], g_up[0, 0], g_down[0, 0],
                      old_up[0, 0, 0], old_down[0, 0, 0], x)
         wg_up, wg_dn, yr, pout = outs[4], outs[5], outs[8], outs[9]
-        y = second(x, pout, wg_up, wg_dn, yr)
-        new_up = w_up - learn_rate[0] * g_up
-        new_down = w_down - learn_rate[0] * g_down
-        return new_up, new_down, y[None, None]
+        role = lax.axis_index("side").astype(jnp.int32)[None]
+        y, new_up, new_down = second(role, learn_rate, x, pout, wg_up, wg_dn, yr,
+                                     w_up[0, 0], g_up[0, 0], w_down[0, 0], g_down[0, 0])
+        return new_up[None, None], new_down[None, None], y[None, None]
 
     return jax.shard_map(
         local_step,

time: 559 us -> 496 us (0.89)
  Pallas kernels: 529 us -> 493 us
  other arithmetic: 20.8 us -> 0 us
  local copies, waits for them, and re-layouts: 6.33 us -> 0 us
    pallas_call x1, Pallas kernels: 489 us -> 434 us  [first(): pl.pallas_call(kern, out_shape=outs, in_specs=[pl.BlockSpec(memory_space=...]
    sub x2 -> x0, other arithmetic: 20.8 us -> none  [the longest x1 15.4 us: local_step(): new_down = w_down - learn_rate[0] * g_down]
    pallas_call x1, Pallas kernels: 39.5 us -> 59.1 us  [second(): pl.pallas_call(kern2, out_shape=(jax.ShapeDtypeStruct((B, D), BF), jax.Sh...]
    unnamed x4 -> x0, local copies, waits for them, and re-layouts: 6.33 us -> none
where the time goes in v2:
time: 496 us; the launch traced here: 495 us
  Pallas kernels  493 us (99%)
    pallas_call x1, Pallas kernels, first(): pl.pallas_call(kern, out_shape=outs, in_specs=[pl.BlockSpec(memory_space=...  434 us
    pallas_call x1, Pallas kernels, second(): pl.pallas_call(kern2, out_shape=(jax.ShapeDtypeStruct((B, D), BF), jax.Sh...  59.1 us

profile of v2, /device:TPU:4, one launch (start us, length us, event | category | flops | bytes accessed | tf_op | source)
XLA Modules:
  0.0 494.8 jit_solution(861962092747603453)
XLA Ops:
  1.3 434.2 %sync_and_mlp.1 = (bf16[384,8960]{1,0:T(8,128)(2,1)}, bf16[8960,384]{1,0:T(8,128)(2,1)}, bf16[384,8960]{1,0:T(8,128)(2,1)}, bf16[8960,384]{1,0:T(8,128)(2,1)}, b...) custom-call(f32[1]{0:T(128)S(6)} %copy.11.lr, ...), custom_call_target="tpu_custom_call" | custom-call | tf_op jit(solution)/shard_map/sync_and_mlp/pallas_call | solution.py:444
  435.5 59.1 %last_pieces.1 = (bf16[8192,1536]{1,0:T(8,128)(2,1)}, f32[384,8960]{1,0:T(8,128)}, f32[8960,384]{1,0:T(8,128)}) custom-call(s32[1]{0:T(128)} %bitcast.role, f32[1]{0:T(128)S(6)} %copy.11.lr, bf16[8192,1536]{1,0:T(8,128)(2,1)} %bitcast.12, f32[7168,1536]{1,0:T(8,128)} %get-tuple-element.10.p_ref, bf16[1536,8960]{1,0:T(8,128)(2,1)} %get-tuple-element.11.wu_ref, ...), custom_call_target="tpu_custom_call" | custom-call | tf_op jit(solution)/shard_map/last_pieces/pallas_call | solution.py:527

commit v3 on v2

--- a/solution.py
+++ b/solution.py
@@ -231,10 +231,19 @@
             sized(0, step_d)
             arrive(0, SMALL)
             w_start(0, SMALL, 0)
+            sized(2, A)
 
             def tile_math(t, xs, s, fc):
                 h = TILE // 2
                 base = pl.multiple_of(t * TILE, TILE)
+                if fc == LARGE:
+                    g = fc // 2
+                    pre_a = dot(xb[xs], wub[s, :, :g])
+                    u_a = gelu_bf16(pre_a)
+                    pre_b = dot(xb[xs], wub[s, :, g:])
+                    u = jnp.concatenate([u_a, gelu_bf16(pre_b)], axis=1)
+                    p[pl.ds(base, TILE)] += dot(u, wdb[s])
+                    return
                 pre_a = dot(xb[xs, :h], wub[s, :, :fc])
                 u_a = gelu_bf16(pre_a)
                 pre_b = dot(xb[xs, h:], wub[s, :, :fc])
@@ -246,44 +255,47 @@
                 s = lax.rem(c, 2)
                 w_wait(c, fc, s)
 
-                @pl.loop(0, NT)
-                def _(t):
-                    i = c * NT + t
-                    xs = lax.rem(i, 2)
-                    x_load(t, xs).wait()
-                    x_load(lax.rem(t + 1, NT), 1 - xs).start()
-
-                    @pl.when(t == 0)
-                    def _():
-                        sized(c + 2, A)
-
-                    @pl.when(t == 1)
+                def load_next(k, fck):
+                    arrive(k, fck)
+
+                    @pl.when(k < N_FIRST)
+                    def _():
+                        w_start(k, fck, 1 - s)
+
+                @pl.loop(0, (NT + 1) // 2)
+                def _(g):
+                    @pl.when(g == 0)
                     def _():
                         sized(c + 2, Bs)
 
-                    @pl.when(t == 2)
+                    @pl.when(g == 1)
                     def _():
                         sized(c + 2, step_c)
 
-                    @pl.when(t == 4)
+                    @pl.when(g == 2)
                     def _():
                         sized(c + 1, step_d)
 
-                    @pl.when(t == 6)
-                    def _():
-                        def load_next(k, fck):
-                            arrive(k, fck)
-
-                            @pl.when(k < N_FIRST)
-                            def _():
-                                w_start(k, fck, 1 - s)
+                    @pl.when(g == 3)
+                    def _():
                         sized(c + 1, load_next)
 
-                    tile_math(t, xs, s, fc)
+                        @pl.when(c + 3 < NCH)
+                        def _():
+                            sized(c + 3, A)
+
+                    @pl.loop(2 * g, jnp.minimum(2 * g + 2, NT))
+                    def _(t):
+                        xs = lax.rem(c * NT + t, 2)
+                        x_load(t, xs).wait()
+                        x_load(lax.rem(t + 1, NT), 1 - xs).start()
+                        tile_math(t, xs, s, fc)
 
                     @pl.when(c == N_FIRST - 1)
                     def _():
-                        p_out(t).start()
+                        @pl.loop(2 * g, jnp.minimum(2 * g + 2, NT))
+                        def _(t):
+                            p_out(t).start()
 
             @pl.loop(0, N_SMALL)
             def _(c):
@@ -293,17 +305,18 @@
             def _(c):
                 chunk(c, LARGE, lambda k, fn: fn(k, LARGE))
 
-            x_load(0, (N_FIRST * NT) % 2).wait()
             for k in range(N_FIRST + 1, NCH):
                 sized(k, step_d)
+            x_load(0, (N_FIRST * NT) % 2).wait()
+            for i in range(NTT):
+                xt_copy(i).wait_send()
+            drain(gen_src)
+            for k in range(N_FIRST + 1, NCH):
                 sized(k, arrive)
             for t in range(NT):
                 p_out(t).wait()
             for i in range(NTT):
                 yt_copy(i).wait_recv()
-            drain(gen_src)
-            for i in range(NTT):
-                xt_copy(i).wait_send()
 
         def trainer(p, st, xb, wub, wdb):
             w_start, w_wait = w_stream(wub, wdb)
@@ -359,8 +372,6 @@
                 sized(k, step_c)
                 sized(k - 1, step_d)
 
-            sized(NCH - 1, step_d)
-
             def x_load(i):
                 return local(xr.at[pl.ds(i * TILE_T, TILE_T)], xb.at[0], lx.at[0])
 
@@ -379,15 +390,19 @@
                 x_load(i).wait()
 
                 def piece(k, fc):
-                    s = lax.rem(k, DEPTH)
+                    s = lax.rem(i * NCH + k, DEPTH)
                     w_wait(k, fc, s)
-                    ahead = lax.rem(k + DEPTH - 1, DEPTH)
+                    ahead = lax.rem(i * NCH + k + DEPTH - 1, DEPTH)
 
                     def nxt(kn, fcn):
                         @pl.when(i == 0)
                         def _():
                             arrive(kn, fcn)
                         w_start(kn, fcn, ahead)
+                    if fc == LARGE:
+                        @pl.when(jnp.logical_and(k == NCH - 6, i == 0))
+                        def _():
+                            step_d(NCH - 1, LARGE)
                     sized(k + DEPTH - 1, nxt)
 
                     @pl.when(jnp.logical_and(k + DEPTH - 1 >= NCH, i < NTT - 1))

time: 496 us -> 494 us (level)
  no operation moved by 1% of the time
where the time goes in v3:
time: 494 us; the launch traced here: 493 us
  Pallas kernels  492 us (100%)
    pallas_call x1, Pallas kernels, first(): pl.pallas_call(kern, out_shape=outs, in_specs=[pl.BlockSpec(memory_space=...  433 us
    pallas_call x1, Pallas kernels, second(): pl.pallas_call(kern2, out_shape=(jax.ShapeDtypeStruct((B, D), BF), jax.Sh...  59.1 us

profile of v3, /device:TPU:4, one launch (start us, length us, event | category | flops | bytes accessed | tf_op | source)
XLA Modules:
  0.0 493.2 jit_solution(11816239285305736017)
XLA Ops:
  1.3 432.6 %sync_and_mlp.1 = (bf16[384,8960]{1,0:T(8,128)(2,1)}, bf16[8960,384]{1,0:T(8,128)(2,1)}, bf16[384,8960]{1,0:T(8,128)(2,1)}, bf16[8960,384]{1,0:T(8,128)(2,1)}, b...) custom-call(f32[1]{0:T(128)S(6)} %copy.11.lr, ...), custom_call_target="tpu_custom_call" | custom-call | tf_op jit(solution)/shard_map/sync_and_mlp/pallas_call | solution.py:459
  433.9 59.1 %last_pieces.1 = (bf16[8192,1536]{1,0:T(8,128)(2,1)}, f32[384,8960]{1,0:T(8,128)}, f32[8960,384]{1,0:T(8,128)}) custom-call(s32[1]{0:T(128)} %bitcast.role, f32[1]{0:T(128)S(6)} %copy.11.lr, bf16[8192,1536]{1,0:T(8,128)(2,1)} %bitcast.12, f32[7168,1536]{1,0:T(8,128)} %get-tuple-element.10.p_ref, bf16[1536,8960]{1,0:T(8,128)(2,1)} %get-tuple-element.11.wu_ref, ...), custom_call_target="tpu_custom_call" | custom-call | tf_op jit(solution)/shard_map/last_pieces/pallas_call | solution.py:542
